TPU v7x, 512 devices: a whole 4x8x8 slice. The times are simulated.
512 devices in a mesh: node: 128 (over z, y, core), rep: 4 (over x).
Axes of the slice: x: 4, y: 8, z: 8, core: 2. Of those that a mesh axis runs over, the one named last changes fastest.
Arguments:
- coords: float32 [3, 65536], P(None, 'node'), may hold values from 0 to 2, as said below
- omega: bfloat16 [65536, 512], P('node', 'rep'), may hold values from -6 to 6
- skeleton: int32 [128, 256], P('node', 'rep'), may hold values from 0 to 65535, as said below
Outputs:
- row_sample: bfloat16 [65536, 512], P('node', 'rep')
- col_sample: float32 [65536, 512], P('node', 'rep')
Inputs may be any that keep to these rules, and one draw needn't show every extreme that they name: `skeleton`: each node's list holds distinct indices, none inside its own points, at most 8 inside the points of any one other node; in every draw one node's points hold exactly 8 indices of every other node's list. `coords`: the first coordinate of point p lies between 2 (p // 512) / 128 and 2 (p // 512 + 1) / 128; the other two lie in [0, 1].
All inputs are finite; a program needn't handle non-finite values.
Results may differ from a plain program's by a relative error of at most 0.0049.
Values may be sent and summed in bfloat16 or wider, within the bound.
A program may use at most 128 MiB of HBM per device.

v0:
```python
import jax
import jax.numpy as jnp
from jax import lax
from jax.sharding import PartitionSpec as P

kernel_scale = 0.0078125
softening = 0.02


def passed_along(block, axis, distance):
    devices = range(lax.axis_size(axis))
    route = [(i - distance, i) for i in devices if i - distance in devices]
    return lax.ppermute(block, axis, route)


def kernel_tile(first_points, target_points):
    squared = (first_points[0][:, None] - target_points[0][None, :]) ** 2
    squared = squared + (first_points[1][:, None] - target_points[1][None, :]) ** 2
    squared = squared + (first_points[2][:, None] - target_points[2][None, :]) ** 2
    return (kernel_scale * lax.rsqrt(squared + softening * softening)).astype(jnp.bfloat16)


def on_device(coords, omega, skeleton):
    node_count = lax.axis_size("node")
    leaf_size = coords.shape[1]
    samp_dev = omega.shape[1]
    listed = lax.all_gather(skeleton, "rep", axis=1, tiled=True)[0]
    rank_size = listed.shape[0]
    capacity = max(8, 2 * rank_size // (node_count - 1))
    owners_of = listed // leaf_size
    local_index = listed % leaf_size
    owner_hits = (owners_of[:, None] == jnp.arange(node_count, dtype=jnp.int32)[None, :]).astype(
        jnp.int32
    )
    slot_rank = jnp.sum((jnp.cumsum(owner_hits, axis=0) - owner_hits) * owner_hits, axis=1)
    flat_slot = owners_of * capacity + slot_rank
    request = (
        jnp.zeros((node_count * capacity,), jnp.int32)
        .at[flat_slot]
        .set(local_index)
        .reshape(node_count, capacity)
    )
    lower_side = (
        passed_along(coords, "node", 1),
        passed_along(omega.astype(jnp.float32), "node", 1).astype(omega.dtype),
    )
    upper_side = (
        passed_along(coords, "node", -1),
        passed_along(omega.astype(jnp.float32), "node", -1).astype(omega.dtype),
    )
    wide_points = jnp.concatenate([lower_side[0], coords, upper_side[0]], axis=1)
    wide_rows = jnp.concatenate([lower_side[1], omega, upper_side[1]], axis=0)
    row_total = jnp.dot(
        kernel_tile(coords, wide_points), wide_rows, preferred_element_type=jnp.float32
    )
    asked_rows = lax.all_to_all(request, "node", split_axis=0, concat_axis=0, tiled=True)
    asked_points = jnp.transpose(coords[:, asked_rows], (1, 0, 2))
    asked_samples = omega[asked_rows]
    got_points, got_samples = (
        lax.all_to_all(asked_points, "node", split_axis=0, concat_axis=0, tiled=True),
        lax.all_to_all(
            asked_samples.astype(jnp.float32), "node", split_axis=0, concat_axis=0, tiled=True
        ).astype(asked_samples.dtype),
    )
    skel_points = jnp.transpose(got_points[owners_of, :, slot_rank])
    skel_tile = kernel_tile(coords, skel_points)
    row_total = row_total + jnp.dot(
        skel_tile, got_samples[owners_of, slot_rank], preferred_element_type=jnp.float32
    )
    transposed = lax.dot_general(
        skel_tile, omega, (((0,), (0,)), ((), ())), preferred_element_type=jnp.float32
    )
    outgoing = (
        jnp.zeros((node_count * capacity, samp_dev), jnp.float32).at[flat_slot].set(transposed)
    )
    incoming = lax.all_to_all(
        outgoing.reshape(node_count, capacity, samp_dev),
        "node",
        split_axis=0,
        concat_axis=0,
        tiled=True,
    )
    col_total = (
        jnp.zeros((leaf_size, samp_dev), jnp.float32)
        .at[asked_rows.reshape(-1)]
        .add(incoming.reshape(-1, samp_dev))
    )
    return (row_total.astype(jnp.bfloat16), col_total)


def solution(mesh):
    in_specs = (P(None, "node"), P("node", "rep"), P("node", "rep"))
    out_specs = (P("node", "rep"), P("node", "rep"))
    return jax.shard_map(
        on_device, mesh=mesh, in_specs=in_specs, out_specs=out_specs, check_vma=False
    )
```

profile of v0, /device:TPU:1, one launch (start us, length us, event | category | flops | bytes accessed | tf_op | source)
XLA Modules:
  0.0 136.3 jit_solution(15671302915424424643)
XLA Ops:
  0.6 1.3 dynamic-slice
  3.3 7.7 %all-reduce = s32[256]{0:T(256)S(1)} all-reduce(s32[256]{0:T(256)S(1)} %bitcast_dynamic-update-slice_fusion), channel_id=1, replica_groups=mesh['node'=128,'rep'=4] {'rep'}, use_global_device_ids=true, to_apply=%add | all-reduce | flops 256 | bytes 2048 | tf_op jit(solution)/shard_map/squeeze | solution.py:27
  11.7 1.4 %scatter_custom_fusion = s32[1024]{0:T(1024)S(1)} fusion(s32[256]{0:T(256)S(1)} %bitcast.70, s32[256]{0:T(256)S(1)} %get-tuple-element.13, s32[]{:T(128)} %constant.26.clone.1), kind=kCustom, calls=%fused_computation.53 | custom fusion | bytes 4100 | tf_op jit(solution)/shard_map/scatter | solution.py:40
  13.8 19.6 %all-to-all-start = ((s32[128,1,8]{2,1,0:T(1,128)}), s32[128,1,8]{2,1,0:T(1,128)S(1)}, u32[]{:S(2)}, u32[]{:S(2)}) async-start(s32[128,1,8]{2,1,0:T(1,128)} %bitcast.12), calls=%async_computation | async-start | bytes 131072 | tf_op jit(solution)/shard_map/all_to_all | solution.py:56
  33.4 3.5 %collective-permute-start = (f32[3,512]{1,0:T(4,128)S(1)}, f32[3,512]{1,0:T(4,128)S(1)}, u32[]{:S(2)}, u32[]{:S(2)}) collective-permute-start(f32[3,512]{1,0:T(4,128)S(1)} %copy-done.1), channel_id=1, source_target_pairs={{0,4},{4,8},{8,12},{12,16},{16,20},{20,24},{24,28},{28,32},{32,36}... | collective-permute-start | bytes 18440 | tf_op jit(solution)/shard_map/ppermute | solution.py:13
  37.0 1.9 %collective-permute-start.1 = (f32[3,512]{1,0:T(4,128)S(1)}, f32[3,512]{1,0:T(4,128)S(1)}, u32[]{:S(2)}, u32[]{:S(2)}) collective-permute-start(f32[3,512]{1,0:T(4,128)S(1)} %copy-done.1), channel_id=1, source_target_pairs={{4,0},{8,4},{12,8},{16,12},{20,16},{24,20},{28,24},{32,28},{36,32}... | collective-permute-start | bytes 18440 | tf_op jit(solution)/shard_map/ppermute | solution.py:13
  38.9 3.6 %collective-permute-start.2 = (bf16[512,128]{1,0:T(8,128)(2,1)S(1)}, bf16[512,128]{1,0:T(8,128)(2,1)S(1)}, u32[]{:S(2)}, u32[]{:S(2)}) collective-permute-start(bf16[512,128]{1,0:T(8,128)(2,1)S(1)} %copy-done), channel_id=1, source_target_pairs={{0,4},{4,8},{8,12},{12,16},{16,20},{20,24},{24,28},{28,32},{32,36}... | collective-permute-start | bytes 393224 | tf_op jit(solution)/shard_map/ppermute | solution.py:13
  42.6 1.9 %collective-permute-start.3 = (bf16[512,128]{1,0:T(8,128)(2,1)S(1)}, bf16[512,128]{1,0:T(8,128)(2,1)S(1)}, u32[]{:S(2)}, u32[]{:S(2)}) collective-permute-start(bf16[512,128]{1,0:T(8,128)(2,1)S(1)} %copy-done), channel_id=1, source_target_pairs={{4,0},{8,4},{12,8},{16,12},{20,16},{24,20},{28,24},{32,28},{36,32}... | collective-permute-start | bytes 393224 | tf_op jit(solution)/shard_map/ppermute | solution.py:13
  45.0 2.8 %gather_fusion = f32[1024,3]{1,0:T(8,128)S(1)} fusion(f32[3,512]{0,1:T(8,128)S(1)} %copy.12, s32[1024]{0:T(1024)S(1)} %broadcast_clamp_fusion), kind=kCustom, calls=%fused_computation | custom fusion | bytes 28672 | tf_op jit(solution)/shard_map/gather | solution.py:57
  47.8 1.5 %copy.13 = f32[128,8,3]{1,2,0:T(4,128)} copy(f32[128,8,3]{2,1,0:T(8,128)S(1)} %bitcast.52) | data formatting | bytes 24576 | tf_op jit(solution)/shard_map/gather | solution.py:57
  49.3 16.1 %all-to-all-start.1 = ((f32[128,3,8]{2,1,0:T(4,128)}), f32[128,3,8]{2,1,0:T(4,128)S(1)}, u32[]{:S(2)}, u32[]{:S(2)}) async-start(f32[128,3,8]{2,1,0:T(4,128)} %bitcast.15), calls=%async_computation.1 | async-start | bytes 524288 | tf_op jit(solution)/shard_map/all_to_all | solution.py:60
  65.4 4.3 %gather_fusion.2 = bf16[1024,128]{1,0:T(8,128)(2,1)} fusion(bf16[512,128]{1,0:T(8,128)(2,1)S(1)} %copy-done, s32[1024]{0:T(1024)S(1)} %broadcast_clamp_fusion), kind=kCustom, calls=%fused_computation.2 | custom fusion | bytes 528384 | tf_op jit(solution)/shard_map/gather | solution.py:58
  69.7 10.9 %all-to-all-done.1 = f32[128,3,8]{2,1,0:T(4,128)S(1)} async-done(((f32[128,3,8]{2,1,0:T(4,128)}), f32[128,3,8]{2,1,0:T(4,128)S(1)}, u32[]{:S(2)}, u32[]{:S(2)}) %all-to-all-start.1) | async-done | bytes 12320 | tf_op jit(solution)/shard_map/all_to_all | solution.py:60
  80.6 5.5 %all-to-all-start.2 = ((bf16[128,8,128]{2,1,0:T(8,128)(2,1)}), bf16[128,8,128]{2,1,0:T(8,128)(2,1)S(1)}, u32[]{:S(2)}, u32[]{:S(2)}) async-start(bf16[128,8,128]{2,1,0:T(8,128)(2,1)} %bitcast.43), calls=%async_computation.2 | async-start | bytes 524288 | tf_op jit(solution)/shard_map/all_to_all | solution.py:61
  86.2 0.8 copy.14
  87.0 1.4 gather_fusion.1
  89.2 1.9 %scatter_custom_fusion.1 = f32[1024,128]{1,0:T(8,128)} fusion(s32[256]{0:T(256)S(1)} %bitcast.71, f32[256,128]{1,0:T(8,128)S(1)} %fusion.12, f32[]{:T(128)} %constant.52.clone.1), kind=kCustom, calls=%fused_computation.20 | custom fusion | bytes 524292 | tf_op jit(solution)/shard_map/scatter | solution.py:74
  91.1 10.4 %all-to-all-done.2 = bf16[128,8,128]{2,1,0:T(8,128)(2,1)S(1)} async-done(((bf16[128,8,128]{2,1,0:T(8,128)(2,1)}), bf16[128,8,128]{2,1,0:T(8,128)(2,1)S(1)}, u32[]{:S(2)}, u32[]{:S(2)}) %all-to-all-start.2) | async-done | bytes 262176 | tf_op jit(solution)/shard_map/all_to_all | solution.py:61
  101.5 5.7 %all-to-all-start.3 = ((f32[128,8,128]{2,1,0:T(8,128)}), f32[128,8,128]{2,1,0:T(8,128)S(1)}, u32[]{:S(2)}, u32[]{:S(2)}) async-start(f32[128,8,128]{2,1,0:T(8,128)} %bitcast.20), calls=%async_computation.3 | async-start | bytes 1048576 | tf_op jit(solution)/shard_map/all_to_all | solution.py:76
  107.8 0.8 reduce.15
  108.8 1.6 %gather_fusion.3 = bf16[256,128]{1,0:T(8,128)(2,1)S(1)} fusion(bf16[128,8,128]{2,1,0:T(8,128)(2,1)S(1)} %all-to-all-done.2, s32[256]{0:T(256)S(1)} %bitcast.50), kind=kCustom, calls=%fused_computation.3 | custom fusion | bytes 133120 | tf_op jit(solution)/shard_map/gather | solution.py:68
  110.8 2.1 %fusion.2 = bf16[512,128]{1,0:T(8,128)(2,1)} fusion(f32[512,128]{1,0:T(8,128)S(1)} %fusion.13, f32[1536]{0:T(1024)S(1)} %get-tuple-element.6, f32[512]{0:T(512)S(1)} %bitcast.69, f32[1536]{0:T(1024)S(1)} %get-tuple-element.7, f32[512]{0:T(512)S(1)} %bitcast.66, f32[1536]{0:T(1024)S(1)} %get-tuple-element.5, f32[512]{0:T(512)S(1)} %bitcast.63, ...), kind=kOutput, calls=%fused_computation.10 | convolution fusion | flops 211288064 | bytes 811008 | tf_op jit(solution)/shard_map/dot_general | solution.py:53
  112.8 15.1 %all-to-all-done.3 = f32[128,8,128]{2,1,0:T(8,128)S(1)} async-done(((f32[128,8,128]{2,1,0:T(8,128)}), f32[128,8,128]{2,1,0:T(8,128)S(1)}, u32[]{:S(2)}, u32[]{:S(2)}) %all-to-all-start.3) | async-done | bytes 524320 | tf_op jit(solution)/shard_map/all_to_all | solution.py:76
  127.9 8.3 %scatter_custom_fusion.2 = f32[512,128]{1,0:T(8,128)} fusion(s32[1024]{0:T(1024)S(1)} %bitcast.60, f32[128,8,128]{2,1,0:T(8,128)S(1)} %all-to-all-done.3, f32[]{:T(128)} %constant.52.clone.1), kind=kCustom, calls=%fused_computation.11 | custom fusion | flops 131072 | bytes 786436 | tf_op jit(solution)/shard_map/scatter-add | solution.py:86
  (40 shorter events, 4.4 us)
Async XLA Ops:
  11.1 22.3 %copy-start.1 = (f32[3,512]{1,0:T(4,128)S(1)}, f32[3,512]{1,0:T(4,128)}, u32[]{:S(2)}) copy-start(f32[3,512]{1,0:T(4,128)} %param.3) | copy-start | bytes 18436
  11.1 27.8 %copy-start = (bf16[512,128]{1,0:T(8,128)(2,1)S(1)}, bf16[512,128]{1,0:T(8,128)(2,1)}, u32[]{:S(2)}) copy-start(bf16[512,128]{1,0:T(8,128)(2,1)} %param.4) | copy-start | bytes 393220
  13.8 31.0 %all-to-all-start = ((s32[128,1,8]{2,1,0:T(1,128)}), s32[128,1,8]{2,1,0:T(1,128)S(1)}, u32[]{:S(2)}, u32[]{:S(2)}) async-start(s32[128,1,8]{2,1,0:T(1,128)} %bitcast.12), calls=%async_computation | async-start | bytes 131072 | tf_op jit(solution)/shard_map/all_to_all | solution.py:56
  33.4 52.7 %collective-permute-start = (f32[3,512]{1,0:T(4,128)S(1)}, f32[3,512]{1,0:T(4,128)S(1)}, u32[]{:S(2)}, u32[]{:S(2)}) collective-permute-start(f32[3,512]{1,0:T(4,128)S(1)} %copy-done.1), channel_id=1, source_target_pairs={{0,4},{4,8},{8,12},{12,16},{16,20},{20,24},{24,28},{28,32},{32,36}... | collective-permute-start | bytes 18440 | tf_op jit(solution)/shard_map/ppermute | solution.py:13
  37.0 70.3 %collective-permute-start.1 = (f32[3,512]{1,0:T(4,128)S(1)}, f32[3,512]{1,0:T(4,128)S(1)}, u32[]{:S(2)}, u32[]{:S(2)}) collective-permute-start(f32[3,512]{1,0:T(4,128)S(1)} %copy-done.1), channel_id=1, source_target_pairs={{4,0},{8,4},{12,8},{16,12},{20,16},{24,20},{28,24},{32,28},{36,32}... | collective-permute-start | bytes 18440 | tf_op jit(solution)/shard_map/ppermute | solution.py:13
  38.9 71.8 %collective-permute-start.2 = (bf16[512,128]{1,0:T(8,128)(2,1)S(1)}, bf16[512,128]{1,0:T(8,128)(2,1)S(1)}, u32[]{:S(2)}, u32[]{:S(2)}) collective-permute-start(bf16[512,128]{1,0:T(8,128)(2,1)S(1)} %copy-done), channel_id=1, source_target_pairs={{0,4},{4,8},{8,12},{12,16},{16,20},{20,24},{24,28},{28,32},{32,36}... | collective-permute-start | bytes 393224 | tf_op jit(solution)/shard_map/ppermute | solution.py:13
  42.6 68.2 %collective-permute-start.3 = (bf16[512,128]{1,0:T(8,128)(2,1)S(1)}, bf16[512,128]{1,0:T(8,128)(2,1)S(1)}, u32[]{:S(2)}, u32[]{:S(2)}) collective-permute-start(bf16[512,128]{1,0:T(8,128)(2,1)S(1)} %copy-done), channel_id=1, source_target_pairs={{4,0},{8,4},{12,8},{16,12},{20,16},{24,20},{28,24},{32,28},{36,32}... | collective-permute-start | bytes 393224 | tf_op jit(solution)/shard_map/ppermute | solution.py:13
  49.3 31.3 %all-to-all-start.1 = ((f32[128,3,8]{2,1,0:T(4,128)}), f32[128,3,8]{2,1,0:T(4,128)S(1)}, u32[]{:S(2)}, u32[]{:S(2)}) async-start(f32[128,3,8]{2,1,0:T(4,128)} %bitcast.15), calls=%async_computation.1 | async-start | bytes 524288 | tf_op jit(solution)/shard_map/all_to_all | solution.py:60
  80.6 20.9 %all-to-all-start.2 = ((bf16[128,8,128]{2,1,0:T(8,128)(2,1)}), bf16[128,8,128]{2,1,0:T(8,128)(2,1)S(1)}, u32[]{:S(2)}, u32[]{:S(2)}) async-start(bf16[128,8,128]{2,1,0:T(8,128)(2,1)} %bitcast.43), calls=%async_computation.2 | async-start | bytes 524288 | tf_op jit(solution)/shard_map/all_to_all | solution.py:61
  101.5 26.4 %all-to-all-start.3 = ((f32[128,8,128]{2,1,0:T(8,128)}), f32[128,8,128]{2,1,0:T(8,128)S(1)}, u32[]{:S(2)}, u32[]{:S(2)}) async-start(f32[128,8,128]{2,1,0:T(8,128)} %bitcast.20), calls=%async_computation.3 | async-start | bytes 1048576 | tf_op jit(solution)/shard_map/all_to_all | solution.py:76
where the time goes:
time: 136 us
  starting transfers between devices  58 us (43%)
  waiting for transfers between devices  36.6 us (27%)
  local copies, waits for them, and re-layouts  19.8 us (15%)
  other arithmetic  9.66 us (7%)
  blocking collectives  7.67 us (6%)
  matrix products  2.95 us (2%)
  between operations  1.56 us (1%)
    all_to_all x1, starting transfers between devices, on_device(): lax.all_to_all(request, 'node', split_axis=0, concat_axis=0, tiled=True)  19.6 us
    all_to_all x1, starting transfers between devices, on_device(): lax.all_to_all(asked_points, 'node', split_axis=0, concat_axis=0, tiled=T...  16.1 us
    all_to_all x1, waiting for transfers between devices, on_device(): lax.all_to_all(outgoing.reshape(node_count, capacity, samp_dev), 'node',...  15.1 us
    ppermute x4, starting transfers between devices, passed_along(): return lax.ppermute(block, axis, route)  11 us
    all_to_all x1, waiting for transfers between devices, on_device(): lax.all_to_all(asked_points, 'node', split_axis=0, concat_axis=0, tiled=T...  10.9 us
    all_to_all x1, waiting for transfers between devices, on_device(): lax.all_to_all(asked_samples.astype(jnp.float32), 'node', split_axis=0, c...  10.4 us
    scatter-add x1, other arithmetic, on_device(): col_total = jnp.zeros((leaf_size, samp_dev), jnp.float32).at[asked_rows.r...  8.35 us
    squeeze x1, blocking collectives, on_device(): listed = lax.all_gather(skeleton, 'rep', axis=1, tiled=True)[0]  7.67 us
  transfers between devices with their start and end apart: 8, of which 4 were waited for; matrix products, arithmetic and copies ran while one was open for 14% of the time, Pallas kernels for 0%

commit v1 on v0

v1 whole, which is shorter than its diff:
```python
import functools

import jax
import jax.numpy as jnp
from jax import lax
from jax.experimental import pallas as pl
from jax.experimental.pallas import tpu as pltpu
from jax.sharding import PartitionSpec as P

MESH = pl.DeviceIdType.MESH
kernel_scale = 0.0078125
softening = 0.02
CAP = 8
F32 = jnp.float32
BF16 = jnp.bfloat16


def dot(a, b):
    return jnp.dot(a, b, preferred_element_type=F32)


def dot_tn(a, b):
    return lax.dot_general(a, b, (((0,), (0,)), ((), ())), preferred_element_type=F32)


def dot_nt(a, b):
    return lax.dot_general(a, b, (((1,), (1,)), ((), ())), preferred_element_type=F32)


def iota(shape, dim):
    return lax.broadcasted_iota(jnp.int32, shape, dim)


def kernel_tile(columns, rows):
    squared = (columns[0] - rows[0]) ** 2
    squared = squared + (columns[1] - rows[1]) ** 2
    squared = squared + (columns[2] - rows[2]) ** 2
    return (kernel_scale * lax.rsqrt(squared + softening * softening)).astype(BF16)


def split3(values):
    high = values.astype(BF16).astype(F32)
    rest = values - high
    middle = rest.astype(BF16).astype(F32)
    return high, middle, rest - middle


def far_first(rows, cols):
    def wrapped(value, size):
        return (value + size // 2 - 1) % size - (size // 2 - 1)

    seen, groups = {(0, 0)}, []
    for a in range(rows):
        for b in range(cols):
            group = []
            for p, q in ((a, b), (-b, a), (-a, -b), (b, -a)):
                pair = (wrapped(p, rows), wrapped(q, cols))
                if pair not in seen:
                    seen.add(pair)
                    group.append(pair)
            if group:
                groups.append(group)
    groups.sort(key=lambda g: -(abs(g[0][0]) + abs(g[0][1])))
    return [pair for group in groups for pair in group]


def level_kernel(
    nodes, reps, coords_ref, omega_ref, skel_ref, row_ref, col_ref,
    lists, reqs, asked, cout, cin, rout, rin, pout, pin, nbc, nbw, own_t, acc, hot,
    send_sem, recv_sem, nb_send, nb_recv,
):
    me, rep = lax.axis_index("node"), lax.axis_index("rep")
    leaf = coords_ref.shape[1]
    samp = omega_ref.shape[1]
    share = skel_ref.shape[1]
    rank_size = share * reps
    slots = nodes * CAP
    z, y, core = me // 16, lax.rem(me // 2, 8), lax.rem(me, 2)
    offsets = far_first(8, 8)

    barrier = pltpu.get_barrier_semaphore()

    @pl.loop(1, reps)
    def _(d):
        pl.semaphore_signal(barrier, inc=1, device_id=(me, lax.rem(rep + d, reps)), device_id_type=MESH)

    @pl.loop(1, nodes)
    def _(d):
        pl.semaphore_signal(barrier, inc=1, device_id=(lax.rem(me + d, nodes), rep), device_id_type=MESH)

    own = coords_ref[...]
    own_rows = [own[k : k + 1, :] for k in range(3)]
    own_t[...] = jnp.transpose(
        jnp.concatenate([own, jnp.zeros((128 - 3, leaf), F32)], axis=0)
    )

    def near(point_rows, sample_rows, first):
        @pl.loop(0, leaf // 128)
        def _(m):
            part = pl.ds(pl.multiple_of(m * 128, 128), 128)
            columns = [own_t[part, k : k + 1] for k in range(3)]
            term = dot(kernel_tile(columns, point_rows), sample_rows)
            acc[part, :] = term if first else acc[part, :] + term

    near(own_rows, omega_ref[...], True)
    asked[me] = jnp.zeros((1, 128), F32)
    cin[me] = jnp.zeros((1, 128), F32)
    rin[me] = jnp.zeros((CAP, samp), BF16)
    pin[me] = jnp.zeros((CAP, samp), BF16)
    lists[rep] = skel_ref[...]

    pl.semaphore_wait(barrier, nodes - 1 + reps - 1)

    for d in range(1, reps):
        pltpu.make_async_remote_copy(
            src_ref=skel_ref, dst_ref=lists.at[rep], send_sem=send_sem.at[0], recv_sem=recv_sem.at[0],
            device_id=(me, lax.rem(rep + d, reps)), device_id_type=MESH,
        ).start()

    nb_copies = []
    for side, step in ((0, 1), (1, nodes - 1)):
        for j, (src, dst) in enumerate(((coords_ref, nbc), (omega_ref, nbw))):
            nb_copies.append(
                pltpu.make_async_remote_copy(
                    src_ref=src, dst_ref=dst.at[side], send_sem=nb_send.at[side, j], recv_sem=nb_recv.at[side, j],
                    device_id=(lax.rem(me + step, nodes), rep), device_id_type=MESH,
                )
            )
    for copy in nb_copies:
        copy.start()

    def await_bytes(ref, count, sem):
        view = ref.at[pl.ds(0, count)]
        pltpu.make_async_copy(view, view, sem).wait()

    def exchange(src, dst, which):
        def send(target):
            pltpu.make_async_remote_copy(
                src_ref=src.at[target], dst_ref=dst.at[me], send_sem=send_sem.at[which], recv_sem=recv_sem.at[which],
                device_id=(target, rep), device_id_type=MESH,
            ).start()

        for dy, dz in offsets:
            base = lax.rem(z + (dz + 8), 8) * 16 + lax.rem(y + (dy + 8), 8) * 2
            send(base + core)
            send(base + 1 - core)
        send(z * 16 + y * 2 + 1 - core)

    await_bytes(lists, reps - 1, recv_sem.at[0])

    listed = jnp.concatenate([lists[r] for r in range(reps)], axis=1)
    owner_row = listed >> 9
    listed_col = jnp.transpose(jnp.broadcast_to(listed.astype(F32), (128, rank_size))).astype(jnp.int32)
    owner_col = listed_col >> 9
    value_col = (listed_col & (leaf - 1)) + 1
    wide_owner = jnp.concatenate([owner_col] * (rank_size // 128), axis=1)
    same = wide_owner == owner_row
    before = jnp.where(same & (iota(same.shape, 1) < iota(same.shape, 0)), 1.0, 0.0).astype(BF16)
    rank_col = dot(before, jnp.ones((rank_size, 128), BF16)).astype(jnp.int32)
    placed = rank_col == iota((rank_size, 128), 1)
    owner_hot = jnp.where(owner_row == iota((nodes, rank_size), 0), 1.0, 0.0).astype(BF16)
    low = jnp.where(placed, (value_col & 255).astype(F32), 0.0).astype(BF16)
    high = jnp.where(placed, (value_col >> 8).astype(F32), 0.0).astype(BF16)
    request = dot(owner_hot, low) + 256.0 * dot(owner_hot, high)
    reqs[...] = request.reshape(nodes, 1, 128)
    exchange(reqs, asked, 1)

    for copy in nb_copies:
        copy.wait_recv()

    @pl.when(me > 0)
    def _():
        side = nbc[0]
        near([side[k : k + 1, :] for k in range(3)], nbw[0], False)

    @pl.when(me < nodes - 1)
    def _():
        side = nbc[1]
        near([side[k : k + 1, :] for k in range(3)], nbw[1], False)

    parts = []
    for k in range(3):
        parts += list(split3(own_rows[k]))
    stack = jnp.concatenate([jnp.concatenate(parts[3 * k : 3 * k + 3] * CAP, axis=0) for k in range(3)], axis=0)
    stack = jnp.concatenate([stack, jnp.zeros((128 - 9 * CAP, leaf), F32)], axis=0)
    lane = iota((128, leaf), 0)
    slot_of = lax.rem(lane, 24) // 3
    tables = [jnp.where(slot_of == s, stack, 0.0).astype(BF16) for s in range(CAP)]

    await_bytes(asked, nodes - 1, recv_sem.at[1])

    wanted = asked[...].reshape(nodes, 128)
    point = (iota((nodes, leaf), 1) + 1).astype(F32)
    answer = jnp.zeros((nodes, 128), F32)
    for s in range(CAP):
        slot_hot = jnp.where(wanted[:, s : s + 1] == point, 1.0, 0.0).astype(BF16)
        answer = answer + dot_nt(slot_hot, tables[s])
    cout[...] = answer.reshape(nodes, 1, 128)
    exchange(cout, cin, 2)

    spread = jnp.broadcast_to(asked[...], (nodes, CAP, 128))
    spread = jnp.where(iota(spread.shape, 2) == iota(spread.shape, 1), spread, 0.0)
    flat = jnp.sum(spread.reshape(slots, 128), axis=1, keepdims=True)
    hot[...] = jnp.where(flat == (iota((slots, leaf), 1) + 1).astype(F32), 1.0, 0.0).astype(BF16)
    rows = dot(hot[...], omega_ref[...])
    rout[...] = rows.reshape(nodes, CAP, samp).astype(BF16)
    exchange(rout, rin, 3)

    flat_col = owner_col * CAP + rank_col
    flat_wide = jnp.concatenate([flat_col] * (slots // 128), axis=1)
    gather_hot = jnp.where(flat_wide == iota((rank_size, slots), 1), 1.0, 0.0).astype(BF16)
    earlier = jnp.where(same & (iota(same.shape, 0) < iota(same.shape, 1)), 1.0, 0.0)
    rank_row = jnp.sum(earlier, axis=0, keepdims=True).astype(jnp.int32)
    flat_row = owner_row * CAP + rank_row
    scatter_hot = jnp.where(flat_row == iota((slots, rank_size), 0), 1.0, 0.0).astype(BF16)
    pick = jnp.where(owner_col == iota((rank_size, 128), 1), 1.0, 0.0).astype(BF16)
    lanes = iota((rank_size, 128), 1)
    mine = lax.rem(lanes, 24) // 3 == rank_col

    await_bytes(cin, nodes - 1, recv_sem.at[2])
    found = dot(pick, cin[...].reshape(nodes, 128).astype(BF16))
    skel_cols = [
        jnp.sum(jnp.where(mine & (lanes // 24 == k), found, 0.0), axis=1, keepdims=True) for k in range(3)
    ]
    skel_tile = kernel_tile(skel_cols, own_rows)
    transposed = dot(skel_tile, omega_ref[...]).astype(BF16)
    pout[...] = dot(scatter_hot, transposed).reshape(nodes, CAP, samp).astype(BF16)
    exchange(pout, pin, 4)

    await_bytes(rin, nodes - 1, recv_sem.at[3])
    got = rin[...].astype(F32).reshape(slots, samp).astype(BF16)
    skel_samples = dot(gather_hot, got).astype(BF16)
    row_ref[...] = (acc[...] + dot_tn(skel_tile, skel_samples)).astype(BF16)

    await_bytes(pin, nodes - 1, recv_sem.at[4])
    incoming = pin[...].astype(F32).reshape(slots, samp).astype(BF16)
    col_ref[...] = dot_tn(hot[...], incoming)

    await_bytes(lists, reps - 1, send_sem.at[0])
    for which, ref in ((1, reqs), (2, cout), (3, rout), (4, pout)):
        await_bytes(ref, nodes - 1, send_sem.at[which])
    for copy in nb_copies:
        copy.wait_send()


def solution(mesh):
    nodes, reps = mesh.shape["node"], mesh.shape["rep"]

    def on_device(coords, omega, skeleton):
        leaf, samp = omega.shape
        share = skeleton.shape[1]
        vmem = pl.BlockSpec(memory_space=pltpu.VMEM)
        return pl.pallas_call(
            functools.partial(level_kernel, nodes, reps),
            out_shape=(
                jax.ShapeDtypeStruct((leaf, samp), BF16),
                jax.ShapeDtypeStruct((leaf, samp), F32),
            ),
            in_specs=[vmem] * 3,
            out_specs=(vmem, vmem),
            scratch_shapes=[
                pltpu.VMEM((reps, 1, share), jnp.int32),
                pltpu.VMEM((nodes, 1, 128), F32),
                pltpu.VMEM((nodes, 1, 128), F32),
                pltpu.VMEM((nodes, 1, 128), F32),
                pltpu.VMEM((nodes, 1, 128), F32),
                pltpu.VMEM((nodes, CAP, samp), BF16),
                pltpu.VMEM((nodes, CAP, samp), BF16),
                pltpu.VMEM((nodes, CAP, samp), BF16),
                pltpu.VMEM((nodes, CAP, samp), BF16),
                pltpu.VMEM((2, 3, leaf), F32),
                pltpu.VMEM((2, leaf, samp), BF16),
                pltpu.VMEM((leaf, 128), F32),
                pltpu.VMEM((leaf, samp), F32),
                pltpu.VMEM((nodes * CAP, leaf), BF16),
                pltpu.SemaphoreType.DMA((5,)),
                pltpu.SemaphoreType.DMA((5,)),
                pltpu.SemaphoreType.DMA((2, 2)),
                pltpu.SemaphoreType.DMA((2, 2)),
            ],
            compiler_params=pltpu.CompilerParams(collective_id=0, has_side_effects=True),
        )(coords, omega, skeleton)

    return jax.shard_map(
        on_device,
        mesh=mesh,
        in_specs=(P(None, "node"), P("node", "rep"), P("node", "rep")),
        out_specs=(P("node", "rep"), P("node", "rep")),
        check_vma=False,
    )
```

time: 136 us -> 52.9 us (0.39)
  starting transfers between devices: 58 us -> 0 us
  Pallas kernels: 0 us -> 49.8 us
  waiting for transfers between devices: 36.6 us -> 0 us
  local copies, waits for them, and re-layouts: 19.8 us -> 2.32 us
  other arithmetic: 9.66 us -> 0 us
  blocking collectives: 7.67 us -> 0 us
  matrix products: 2.95 us -> 0 us
    pallas_call x0 -> x1, Pallas kernels: none -> 49.8 us  [on_device(): pl.pallas_call(functools.partial(level_kernel, nodes, reps), out_shape=(j...]
    all_to_all x4 -> x0, starting transfers between devices: 47 us -> none  [the longest x1 19.6 us: on_device(): lax.all_to_all(request, 'node', split_axis=0, concat_axis=0, tiled=True)]
    all_to_all x4 -> x0, waiting for transfers between devices: 36.6 us -> none  [the longest x1 15.1 us: on_device(): lax.all_to_all(outgoing.reshape(node_count, capacity, samp_dev), 'node',...]
    gather x5 -> x0, local copies, waits for them, and re-layouts: 11.6 us -> none  [the longest x2 4.32 us: on_device(): asked_points = jnp.transpose(coords[:, asked_rows], (1, 0, 2))]
    ppermute x4 -> x0, starting transfers between devices: 11 us -> none  [passed_along(): return lax.ppermute(block, axis, route)]
    scatter-add x1 -> x0, other arithmetic: 8.35 us -> none  [on_device(): col_total = jnp.zeros((leaf_size, samp_dev), jnp.float32).at[asked_rows.r...]
    squeeze x1 -> x0, blocking collectives: 7.67 us -> none  [on_device(): listed = lax.all_gather(skeleton, 'rep', axis=1, tiled=True)[0]]
    scatter x2 -> x0, local copies, waits for them, and re-layouts: 3.33 us -> none  [the longest x1 1.92 us: on_device(): jnp.zeros((node_count * capacity, samp_dev), jnp.float32).at[flat_slot]]
  transfers between devices with their start and end apart: 8 -> 0, of which waited for: 4 -> 0; matrix products, arithmetic and copies ran while one was open for 14% -> 0% of each run, Pallas kernels for 0% -> 0%
where the time goes in v1:
time: 52.9 us; the launch traced here: 52.7 us
  Pallas kernels  49.8 us (94%)
  local copies, waits for them, and re-layouts  2.32 us (4%)
  between operations  0.65 us (1%)
    pallas_call x1, Pallas kernels, on_device(): pl.pallas_call(functools.partial(level_kernel, nodes, reps), out_shape=(j...  49.8 us
    unnamed x4, local copies, waits for them, and re-layouts  2.32 us

profile of v1, /device:TPU:1, one launch (start us, length us, event | category | flops | bytes accessed | tf_op | source)
XLA Modules:
  0.0 52.7 jit_solution(173496432914368068)
XLA Ops:
  0.6 49.8 %shard_map.50 = (bf16[512,128]{1,0:T(8,128)(2,1)}, f32[512,128]{1,0:T(8,128)}) custom-call(f32[3,512]{1,0:T(4,128)} %coords_ref.1, bf16[512,128]{1,0:T(8,128)(2,1)} %omega_ref.1, s32[1,64]{1,0:T(1,128)} %skel_ref.1), custom_call_target="tpu_custom_call" | custom-call | tf_op jit(solution)/shard_map/pallas_call | solution.py:253
  50.4 0.0 copy-start
  50.4 1.6 %copy.7 = bf16[512,128]{1,0:T(8,128)(2,1)} copy(bf16[512,128]{1,0:T(8,128)(2,1)} %get-tuple-element.4) | data formatting | bytes 262144
  52.0 0.0 copy-done
  52.0 0.7 %copy.8 = f32[512,128]{1,0:T(8,128)} copy(f32[512,128]{1,0:T(8,128)S(1)} %copy-done) | data formatting | bytes 524288
Async XLA Ops:
  50.4 1.6 %copy-start = (f32[512,128]{1,0:T(8,128)S(1)}, f32[512,128]{1,0:T(8,128)}, u32[]{:S(2)}) copy-start(f32[512,128]{1,0:T(8,128)} %get-tuple-element.5) | copy-start | bytes 786436

commit v2 on v1

--- a/solution.py
+++ b/solution.py
@@ -11,6 +11,7 @@
 kernel_scale = 0.0078125
 softening = 0.02
 CAP = 8
+VMEM_LIMIT = 24 << 20
 F32 = jnp.float32
 BF16 = jnp.bfloat16
 
@@ -65,9 +66,9 @@
 
 
 def level_kernel(
-    nodes, reps, coords_ref, omega_ref, skel_ref, row_ref, col_ref,
-    lists, reqs, asked, cout, cin, rout, rin, pout, pin, nbc, nbw, own_t, acc, hot,
-    send_sem, recv_sem, nb_send, nb_recv,
+    nodes, reps, coords_hbm, omega_hbm, skel_hbm, row_ref, pin, spots,
+    coords_ref, omega_ref, skel_ref, lists, reqs, asked, cout, cin, rout, rin, pout, nbc, nbw, own_t, acc, hot,
+    load_sem, plane_sem, send_sem, recv_sem, nb_send, nb_recv,
 ):
     me, rep = lax.axis_index("node"), lax.axis_index("rep")
     leaf = coords_ref.shape[1]
@@ -84,9 +85,23 @@
     def _(d):
         pl.semaphore_signal(barrier, inc=1, device_id=(me, lax.rem(rep + d, reps)), device_id_type=MESH)
 
-    @pl.loop(1, nodes)
+    @pl.loop(1, 8)
     def _(d):
-        pl.semaphore_signal(barrier, inc=1, device_id=(lax.rem(me + d, nodes), rep), device_id_type=MESH)
+        pl.semaphore_signal(barrier, inc=1, device_id=(lax.rem(me + 16 * d, nodes), rep), device_id_type=MESH)
+
+    @pl.loop(1, 16)
+    def _(d):
+        peer = z * 16 + lax.rem(lax.rem(me, 16) + d, 16)
+        pl.semaphore_signal(barrier, inc=1, device_id=(peer, rep), device_id_type=MESH)
+
+    loads = [
+        pltpu.make_async_copy(src, dst, load_sem.at[k])
+        for k, (src, dst) in enumerate(((skel_hbm, skel_ref), (coords_hbm, coords_ref), (omega_hbm, omega_ref)))
+    ]
+    for load in loads:
+        load.start()
+    for load in loads:
+        load.wait()
 
     own = coords_ref[...]
     own_rows = [own[k : k + 1, :] for k in range(3)]
@@ -109,7 +124,7 @@
     pin[me] = jnp.zeros((CAP, samp), BF16)
     lists[rep] = skel_ref[...]
 
-    pl.semaphore_wait(barrier, nodes - 1 + reps - 1)
+    pl.semaphore_wait(barrier, reps - 1 + 7 + 15)
 
     for d in range(1, reps):
         pltpu.make_async_remote_copy(
@@ -126,8 +141,10 @@
                     device_id=(lax.rem(me + step, nodes), rep), device_id_type=MESH,
                 )
             )
-    for copy in nb_copies:
-        copy.start()
+
+    @pl.loop(1, 8)
+    def _(d):
+        pl.semaphore_signal(plane_sem, inc=1, device_id=(lax.rem(me + 16 * d, nodes), rep), device_id_type=MESH)
 
     def await_bytes(ref, count, sem):
         view = ref.at[pl.ds(0, count)]
@@ -163,20 +180,10 @@
     high = jnp.where(placed, (value_col >> 8).astype(F32), 0.0).astype(BF16)
     request = dot(owner_hot, low) + 256.0 * dot(owner_hot, high)
     reqs[...] = request.reshape(nodes, 1, 128)
+    pl.semaphore_wait(plane_sem, 7)
     exchange(reqs, asked, 1)
-
     for copy in nb_copies:
-        copy.wait_recv()
-
-    @pl.when(me > 0)
-    def _():
-        side = nbc[0]
-        near([side[k : k + 1, :] for k in range(3)], nbw[0], False)
-
-    @pl.when(me < nodes - 1)
-    def _():
-        side = nbc[1]
-        near([side[k : k + 1, :] for k in range(3)], nbw[1], False)
+        copy.start()
 
     parts = []
     for k in range(3):
@@ -186,6 +193,14 @@
     lane = iota((128, leaf), 0)
     slot_of = lax.rem(lane, 24) // 3
     tables = [jnp.where(slot_of == s, stack, 0.0).astype(BF16) for s in range(CAP)]
+
+    for copy in nb_copies:
+        copy.wait_recv()
+
+    @pl.when(me > 0)
+    def _():
+        side = nbc[0]
+        near([side[k : k + 1, :] for k in range(3)], nbw[0], False)
 
     await_bytes(asked, nodes - 1, recv_sem.at[1])
 
@@ -217,6 +232,11 @@
     lanes = iota((rank_size, 128), 1)
     mine = lax.rem(lanes, 24) // 3 == rank_col
 
+    @pl.when(me < nodes - 1)
+    def _():
+        side = nbc[1]
+        near([side[k : k + 1, :] for k in range(3)], nbw[1], False)
+
     await_bytes(cin, nodes - 1, recv_sem.at[2])
     found = dot(pick, cin[...].reshape(nodes, 128).astype(BF16))
     skel_cols = [
@@ -226,21 +246,34 @@
     transposed = dot(skel_tile, omega_ref[...]).astype(BF16)
     pout[...] = dot(scatter_hot, transposed).reshape(nodes, CAP, samp).astype(BF16)
     exchange(pout, pin, 4)
+    spots[...] = jnp.transpose(hot[...])
 
     await_bytes(rin, nodes - 1, recv_sem.at[3])
     got = rin[...].astype(F32).reshape(slots, samp).astype(BF16)
     skel_samples = dot(gather_hot, got).astype(BF16)
     row_ref[...] = (acc[...] + dot_tn(skel_tile, skel_samples)).astype(BF16)
-
-    await_bytes(pin, nodes - 1, recv_sem.at[4])
-    incoming = pin[...].astype(F32).reshape(slots, samp).astype(BF16)
-    col_ref[...] = dot_tn(hot[...], incoming)
 
     await_bytes(lists, reps - 1, send_sem.at[0])
     for which, ref in ((1, reqs), (2, cout), (3, rout), (4, pout)):
         await_bytes(ref, nodes - 1, send_sem.at[which])
     for copy in nb_copies:
         copy.wait_send()
+    await_bytes(pin, nodes - 1, recv_sem.at[4])
+
+
+def finish_kernel(row_ref, pin, spots, row_hbm, col_hbm, incoming, col_ref, sems):
+    leaf = row_ref.shape[0]
+    copies = [pltpu.make_async_copy(row_ref, row_hbm, sems.at[0])]
+    copies[0].start()
+    incoming[...] = pin[...].astype(F32).reshape(incoming.shape).astype(BF16)
+    step = leaf // 2
+    for k in range(2):
+        part = pl.ds(k * step, step)
+        col_ref[part, :] = dot(spots[part, :], incoming[...])
+        copies.append(pltpu.make_async_copy(col_ref.at[part], col_hbm.at[part], sems.at[1 + k]))
+        copies[-1].start()
+    for copy in copies:
+        copy.wait()
 
 
 def solution(mesh):
@@ -250,15 +283,20 @@
         leaf, samp = omega.shape
         share = skeleton.shape[1]
         vmem = pl.BlockSpec(memory_space=pltpu.VMEM)
-        return pl.pallas_call(
+        anywhere = pl.BlockSpec(memory_space=pl.ANY)
+        row, incoming, spots = pl.pallas_call(
             functools.partial(level_kernel, nodes, reps),
             out_shape=(
                 jax.ShapeDtypeStruct((leaf, samp), BF16),
-                jax.ShapeDtypeStruct((leaf, samp), F32),
+                jax.ShapeDtypeStruct((nodes, CAP, samp), BF16),
+                jax.ShapeDtypeStruct((leaf, nodes * CAP), BF16),
             ),
-            in_specs=[vmem] * 3,
-            out_specs=(vmem, vmem),
+            in_specs=[pl.BlockSpec(memory_space=pltpu.HBM)] * 3,
+            out_specs=(vmem,) * 3,
             scratch_shapes=[
+                pltpu.VMEM(coords.shape, F32),
+                pltpu.VMEM((leaf, samp), BF16),
+                pltpu.VMEM((1, share), jnp.int32),
                 pltpu.VMEM((reps, 1, share), jnp.int32),
                 pltpu.VMEM((nodes, 1, 128), F32),
                 pltpu.VMEM((nodes, 1, 128), F32),
@@ -267,19 +305,37 @@
                 pltpu.VMEM((nodes, CAP, samp), BF16),
                 pltpu.VMEM((nodes, CAP, samp), BF16),
                 pltpu.VMEM((nodes, CAP, samp), BF16),
-                pltpu.VMEM((nodes, CAP, samp), BF16),
                 pltpu.VMEM((2, 3, leaf), F32),
                 pltpu.VMEM((2, leaf, samp), BF16),
                 pltpu.VMEM((leaf, 128), F32),
                 pltpu.VMEM((leaf, samp), F32),
                 pltpu.VMEM((nodes * CAP, leaf), BF16),
+                pltpu.SemaphoreType.DMA((3,)),
+                pltpu.SemaphoreType.REGULAR,
                 pltpu.SemaphoreType.DMA((5,)),
                 pltpu.SemaphoreType.DMA((5,)),
                 pltpu.SemaphoreType.DMA((2, 2)),
                 pltpu.SemaphoreType.DMA((2, 2)),
             ],
-            compiler_params=pltpu.CompilerParams(collective_id=0, has_side_effects=True),
+            compiler_params=pltpu.CompilerParams(
+                collective_id=0, has_side_effects=True, vmem_limit_bytes=VMEM_LIMIT
+            ),
         )(coords, omega, skeleton)
+        return pl.pallas_call(
+            finish_kernel,
+            out_shape=(
+                jax.ShapeDtypeStruct((leaf, samp), BF16),
+                jax.ShapeDtypeStruct((leaf, samp), F32),
+            ),
+            in_specs=[vmem] * 3,
+            out_specs=(anywhere,) * 2,
+            scratch_shapes=[
+                pltpu.VMEM((nodes * CAP, samp), BF16),
+                pltpu.VMEM((leaf, samp), F32),
+                pltpu.SemaphoreType.DMA((3,)),
+            ],
+            compiler_params=pltpu.CompilerParams(vmem_limit_bytes=VMEM_LIMIT),
+        )(row, incoming, spots)
 
     return jax.shard_map(
         on_device,

time: 52.9 us -> 49.9 us (0.943)
  Pallas kernels: 49.8 us -> 46.8 us
    pallas_call x1, Pallas kernels: 49.8 us -> 45.6 us  [on_device(): pl.pallas_call(functools.partial(level_kernel, nodes, reps), out_shape=(j...]
    pallas_call x0 -> x1, Pallas kernels: none -> 1.15 us  [on_device(): pl.pallas_call(finish_kernel, out_shape=(jax.ShapeDtypeStruct((leaf, samp...]
    unnamed x4 -> x6, local copies, waits for them, and re-layouts: 2.32 us -> 2.25 us
where the time goes in v2:
time: 49.9 us; the launch traced here: 49.7 us
  Pallas kernels  46.8 us (94%)
  local copies, waits for them, and re-layouts  2.25 us (5%)
  between operations  0.65 us (1%)
    pallas_call x1, Pallas kernels, on_device(): pl.pallas_call(functools.partial(level_kernel, nodes, reps), out_shape=(j...  45.6 us
    unnamed x6, local copies, waits for them, and re-layouts  2.25 us
    pallas_call x1, Pallas kernels, on_device(): pl.pallas_call(finish_kernel, out_shape=(jax.ShapeDtypeStruct((leaf, samp...  1.15 us

profile of v2, /device:TPU:1, one launch (start us, length us, event | category | flops | bytes accessed | tf_op | source)
XLA Modules:
  0.0 49.7 jit_solution(5766780725206522015)
XLA Ops:
  0.6 0.0 copy-start
  0.6 0.9 %copy-done = bf16[512,128]{1,0:T(8,128)(2,1)S(1)} copy-done((bf16[512,128]{1,0:T(8,128)(2,1)S(1)}, bf16[512,128]{1,0:T(8,128)(2,1)}, u32[]{:S(2)}) %copy-start) | copy-done | bytes 131096
  1.5 0.0 copy-start.1
  1.5 0.7 %copy-done.1 = f32[3,512]{1,0:T(4,128)S(1)} copy-done((f32[3,512]{1,0:T(4,128)S(1)}, f32[3,512]{1,0:T(4,128)}, u32[]{:S(2)}) %copy-start.1) | copy-done | bytes 6168
  2.2 0.0 copy-start.2
  2.2 0.7 %copy-done.2 = s32[1,64]{1,0:T(1,128)S(1)} copy-done((s32[1,64]{1,0:T(1,128)S(1)}, s32[1,64]{1,0:T(1,128)}, u32[]{:S(2)}) %copy-start.2) | copy-done | bytes 280
  2.9 45.6 %shard_map.50 = (bf16[512,128]{1,0:T(8,128)(2,1)S(1)}, bf16[128,8,128]{2,1,0:T(8,128)(2,1)S(1)}, bf16[512,1024]{1,0:T(8,128)(2,1)S(1)}) custom-call(f32[3,512]{1,0:T(4,128)S(1)} %copy-done.1, bf16[512,128]{1,0:T(8,128)(2,1)S(1)} %copy-done, s32[1,64]{1,0:T(1,128)S(1)} %copy-done.2), custom_call_target="tpu_custom_call" | custom-call | tf_op jit(solution)/shard_map/pallas_call | solution.py:287
  48.5 1.2 %shard_map.51 = (bf16[512,128]{1,0:T(8,128)(2,1)}, f32[512,128]{1,0:T(8,128)}) custom-call(bf16[512,128]{1,0:T(8,128)(2,1)S(1)} %get-tuple-element.5.row_ref, bf16[128,8,128]{2,1,0:T(8,128)(2,1)S(1)} %get-tuple-element.6.pin, bf16[512,1024]{1,0:T(8,128)(2,1)S(1)} %get-tuple-element.7.spots), custom_call_target="tpu_custom_call" | custom-call | tf_op jit(solution)/shard_map/pallas_call | solution.py:324
Async XLA Ops:
  0.6 0.9 %copy-start = (bf16[512,128]{1,0:T(8,128)(2,1)S(1)}, bf16[512,128]{1,0:T(8,128)(2,1)}, u32[]{:S(2)}) copy-start(bf16[512,128]{1,0:T(8,128)(2,1)} %omega_hbm.1) | copy-start | bytes 393220
  1.5 0.7 %copy-start.1 = (f32[3,512]{1,0:T(4,128)S(1)}, f32[3,512]{1,0:T(4,128)}, u32[]{:S(2)}) copy-start(f32[3,512]{1,0:T(4,128)} %coords_hbm.1) | copy-start | bytes 18436
  2.2 0.7 %copy-start.2 = (s32[1,64]{1,0:T(1,128)S(1)}, s32[1,64]{1,0:T(1,128)}, u32[]{:S(2)}) copy-start(s32[1,64]{1,0:T(1,128)} %skel_hbm.1) | copy-start | bytes 772

commit v3 on v2

--- a/solution.py
+++ b/solution.py
@@ -11,6 +11,10 @@
 kernel_scale = 0.0078125
 softening = 0.02
 CAP = 8
+LINE = 16
+Y_ORDER = (8, 7, 9, 6, 10, 5, 11, 4, 12, 3, 13, 2, 14, 1, 15)
+Z_ORDER = (4, 3, 5, 2, 6, 1, 7)
+ROWS_FIRST = True
 VMEM_LIMIT = 24 << 20
 F32 = jnp.float32
 BF16 = jnp.bfloat16
@@ -67,7 +71,8 @@
 
 def level_kernel(
     nodes, reps, coords_hbm, omega_hbm, skel_hbm, row_ref, pin, spots,
-    coords_ref, omega_ref, skel_ref, lists, reqs, asked, cout, cin, rout, rin, pout, nbc, nbw, own_t, acc, hot,
+    coords_ref, omega_ref, skel_ref, lists, reqs, asked, zreq, zasked, zout, zin, line, rout, rin, pout,
+    nbc, nbw, own_t, own_wide, omega_t, table, acc, hot, scatter_hot, tile,
     load_sem, plane_sem, send_sem, recv_sem, nb_send, nb_recv,
 ):
     me, rep = lax.axis_index("node"), lax.axis_index("rep")
@@ -76,8 +81,16 @@
     share = skel_ref.shape[1]
     rank_size = share * reps
     slots = nodes * CAP
-    z, y, core = me // 16, lax.rem(me // 2, 8), lax.rem(me, 2)
+    z, y, core = me // LINE, lax.rem(me // 2, LINE // 2), lax.rem(me, 2)
+    spot = lax.rem(me, LINE)
+    planes = nodes // LINE
     offsets = far_first(8, 8)
+
+    def z_peer(d):
+        return lax.rem(z + d, planes)
+
+    def y_peer(d):
+        return z * LINE + lax.rem(spot + d, LINE)
 
     barrier = pltpu.get_barrier_semaphore()
 
@@ -85,14 +98,13 @@
     def _(d):
         pl.semaphore_signal(barrier, inc=1, device_id=(me, lax.rem(rep + d, reps)), device_id_type=MESH)
 
-    @pl.loop(1, 8)
+    @pl.loop(1, LINE)
     def _(d):
-        pl.semaphore_signal(barrier, inc=1, device_id=(lax.rem(me + 16 * d, nodes), rep), device_id_type=MESH)
-
-    @pl.loop(1, 16)
+        pl.semaphore_signal(barrier, inc=1, device_id=(y_peer(d), rep), device_id_type=MESH)
+
+    @pl.loop(1, planes)
     def _(d):
-        peer = z * 16 + lax.rem(lax.rem(me, 16) + d, 16)
-        pl.semaphore_signal(barrier, inc=1, device_id=(peer, rep), device_id_type=MESH)
+        pl.semaphore_signal(barrier, inc=1, device_id=(z_peer(d) * LINE + spot, rep), device_id_type=MESH)
 
     loads = [
         pltpu.make_async_copy(src, dst, load_sem.at[k])
@@ -100,37 +112,46 @@
     ]
     for load in loads:
         load.start()
-    for load in loads:
-        load.wait()
-
-    own = coords_ref[...]
-    own_rows = [own[k : k + 1, :] for k in range(3)]
-    own_t[...] = jnp.transpose(
-        jnp.concatenate([own, jnp.zeros((128 - 3, leaf), F32)], axis=0)
-    )
-
-    def near(point_rows, sample_rows, first):
-        @pl.loop(0, leaf // 128)
-        def _(m):
-            part = pl.ds(pl.multiple_of(m * 128, 128), 128)
-            columns = [own_t[part, k : k + 1] for k in range(3)]
-            term = dot(kernel_tile(columns, point_rows), sample_rows)
-            acc[part, :] = term if first else acc[part, :] + term
-
-    near(own_rows, omega_ref[...], True)
-    asked[me] = jnp.zeros((1, 128), F32)
-    cin[me] = jnp.zeros((1, 128), F32)
-    rin[me] = jnp.zeros((CAP, samp), BF16)
-    pin[me] = jnp.zeros((CAP, samp), BF16)
-    lists[rep] = skel_ref[...]
-
-    pl.semaphore_wait(barrier, reps - 1 + 7 + 15)
+    loads[0].wait()
+    loads[1].wait()
+    pl.semaphore_wait(barrier, reps - 1 + LINE - 1 + planes - 1)
 
     for d in range(1, reps):
         pltpu.make_async_remote_copy(
             src_ref=skel_ref, dst_ref=lists.at[rep], send_sem=send_sem.at[0], recv_sem=recv_sem.at[0],
             device_id=(me, lax.rem(rep + d, reps)), device_id_type=MESH,
         ).start()
+    for d in Y_ORDER:
+        pltpu.make_async_remote_copy(
+            src_ref=coords_ref, dst_ref=line.at[spot], send_sem=send_sem.at[5], recv_sem=recv_sem.at[5],
+            device_id=(y_peer(d), rep), device_id_type=MESH,
+        ).start()
+
+    @pl.loop(1, planes)
+    def _(d):
+        pl.semaphore_signal(plane_sem, inc=1, device_id=(z_peer(d) * LINE + spot, rep), device_id_type=MESH)
+
+    loads[2].wait()
+    lists[rep] = skel_ref[...]
+    line[spot] = coords_ref[...]
+    asked[me] = jnp.zeros((1, 128), F32)
+    rin[me] = jnp.zeros((CAP, samp), BF16)
+    pin[me] = jnp.zeros((CAP, samp), BF16)
+    own = coords_ref[...]
+    own_rows = [own[k : k + 1, :] for k in range(3)]
+    own_t[...] = jnp.transpose(jnp.concatenate([own, jnp.zeros((128 - 3, leaf), F32)], axis=0))
+    for k in range(3):
+        own_wide[k] = jnp.broadcast_to(own_t[:, k : k + 1], (leaf, 128))
+
+    def near(point_rows, sample_rows, first):
+        @pl.loop(0, leaf // 128)
+        def _(m):
+            part = pl.ds(pl.multiple_of(m * 128, 128), 128)
+            columns = [jnp.concatenate([own_wide[k, part, :]] * (leaf // 128), axis=1) for k in range(3)]
+            term = dot(kernel_tile(columns, point_rows), sample_rows)
+            acc[part, :] = term if first else acc[part, :] + term
+
+    near(own_rows, omega_ref[...], True)
 
     nb_copies = []
     for side, step in ((0, 1), (1, nodes - 1)):
@@ -142,10 +163,6 @@
                 )
             )
 
-    @pl.loop(1, 8)
-    def _(d):
-        pl.semaphore_signal(plane_sem, inc=1, device_id=(lax.rem(me + 16 * d, nodes), rep), device_id_type=MESH)
-
     def await_bytes(ref, count, sem):
         view = ref.at[pl.ds(0, count)]
         pltpu.make_async_copy(view, view, sem).wait()
@@ -158,10 +175,17 @@
             ).start()
 
         for dy, dz in offsets:
-            base = lax.rem(z + (dz + 8), 8) * 16 + lax.rem(y + (dy + 8), 8) * 2
+            base = lax.rem(z + (dz + 8), 8) * LINE + lax.rem(y + (dy + 8), 8) * 2
             send(base + core)
             send(base + 1 - core)
-        send(z * 16 + y * 2 + 1 - core)
+        send(z * LINE + y * 2 + 1 - core)
+
+    def z_exchange(src, dst, which):
+        for d in Z_ORDER:
+            pltpu.make_async_remote_copy(
+                src_ref=src.at[z_peer(d)], dst_ref=dst.at[z], send_sem=send_sem.at[which], recv_sem=recv_sem.at[which],
+                device_id=(z_peer(d) * LINE + spot, rep), device_id_type=MESH,
+            ).start()
 
     await_bytes(lists, reps - 1, recv_sem.at[0])
 
@@ -174,52 +198,52 @@
     same = wide_owner == owner_row
     before = jnp.where(same & (iota(same.shape, 1) < iota(same.shape, 0)), 1.0, 0.0).astype(BF16)
     rank_col = dot(before, jnp.ones((rank_size, 128), BF16)).astype(jnp.int32)
-    placed = rank_col == iota((rank_size, 128), 1)
+    low_col = (value_col & 255).astype(F32)
+    high_col = (value_col >> 8).astype(F32)
+
+    def requests(lane_col, owner_hot):
+        placed = lane_col == iota((rank_size, 128), 1)
+        low = jnp.where(placed, low_col, 0.0).astype(BF16)
+        high = jnp.where(placed, high_col, 0.0).astype(BF16)
+        return dot(owner_hot, low) + 256.0 * dot(owner_hot, high)
+
+    z_hot = jnp.where((owner_row >> 4) == iota((16, rank_size), 0), 1.0, 0.0).astype(BF16)
+    z_request = requests((owner_col & (LINE - 1)) * CAP + rank_col, z_hot)
+    for i in range(planes):
+        zreq[i] = z_request[i : i + 1, :]
+    z_exchange(zreq, zasked, 2)
+    zasked[z] = zreq[z]
+
     owner_hot = jnp.where(owner_row == iota((nodes, rank_size), 0), 1.0, 0.0).astype(BF16)
-    low = jnp.where(placed, (value_col & 255).astype(F32), 0.0).astype(BF16)
-    high = jnp.where(placed, (value_col >> 8).astype(F32), 0.0).astype(BF16)
-    request = dot(owner_hot, low) + 256.0 * dot(owner_hot, high)
-    reqs[...] = request.reshape(nodes, 1, 128)
-    pl.semaphore_wait(plane_sem, 7)
+    reqs[...] = requests(rank_col, owner_hot).reshape(nodes, 1, 128)
+    pl.semaphore_wait(plane_sem, planes - 1)
     exchange(reqs, asked, 1)
     for copy in nb_copies:
         copy.start()
 
-    parts = []
+    await_bytes(line, LINE - 1, recv_sem.at[5])
     for k in range(3):
-        parts += list(split3(own_rows[k]))
-    stack = jnp.concatenate([jnp.concatenate(parts[3 * k : 3 * k + 3] * CAP, axis=0) for k in range(3)], axis=0)
-    stack = jnp.concatenate([stack, jnp.zeros((128 - 9 * CAP, leaf), F32)], axis=0)
-    lane = iota((128, leaf), 0)
-    slot_of = lax.rem(lane, 24) // 3
-    tables = [jnp.where(slot_of == s, stack, 0.0).astype(BF16) for s in range(CAP)]
-
-    for copy in nb_copies:
-        copy.wait_recv()
-
-    @pl.when(me > 0)
-    def _():
-        side = nbc[0]
-        near([side[k : k + 1, :] for k in range(3)], nbw[0], False)
-
-    await_bytes(asked, nodes - 1, recv_sem.at[1])
-
-    wanted = asked[...].reshape(nodes, 128)
-    point = (iota((nodes, leaf), 1) + 1).astype(F32)
-    answer = jnp.zeros((nodes, 128), F32)
-    for s in range(CAP):
-        slot_hot = jnp.where(wanted[:, s : s + 1] == point, 1.0, 0.0).astype(BF16)
-        answer = answer + dot_nt(slot_hot, tables[s])
-    cout[...] = answer.reshape(nodes, 1, 128)
-    exchange(cout, cin, 2)
-
-    spread = jnp.broadcast_to(asked[...], (nodes, CAP, 128))
-    spread = jnp.where(iota(spread.shape, 2) == iota(spread.shape, 1), spread, 0.0)
-    flat = jnp.sum(spread.reshape(slots, 128), axis=1, keepdims=True)
-    hot[...] = jnp.where(flat == (iota((slots, leaf), 1) + 1).astype(F32), 1.0, 0.0).astype(BF16)
-    rows = dot(hot[...], omega_ref[...])
-    rout[...] = rows.reshape(nodes, CAP, samp).astype(BF16)
-    exchange(rout, rin, 3)
+        for part, values in enumerate(split3(jnp.concatenate([line[n, k : k + 1, :] for n in range(LINE)], axis=0))):
+            table[pl.ds((3 * k + part) * LINE, LINE), :] = values.astype(BF16)
+
+    await_bytes(zasked, planes - 1, recv_sem.at[2])
+    width = 256
+    for c in range(slots // width):
+        wanted = jnp.concatenate([zasked[2 * c], zasked[2 * c + 1]], axis=1)
+        point_hot = jnp.where(wanted == (iota((leaf, width), 0) + 1).astype(F32), 1.0, 0.0).astype(BF16)
+        found = dot(table[...], point_hot)
+        own_node = lax.rem(iota((3 * LINE, width), 0), LINE) == lax.rem(iota((3 * LINE, width), 1) // CAP, LINE)
+        answer = jnp.concatenate(
+            [
+                jnp.sum(jnp.where(own_node, found[3 * LINE * k : 3 * LINE * (k + 1)], 0.0), axis=0, keepdims=True)
+                for k in range(3)
+            ],
+            axis=0,
+        )
+        zout[2 * c] = answer[:, :128]
+        zout[2 * c + 1] = answer[:, 128:]
+    z_exchange(zout, zin, 6)
+    zin[z] = zout[z]
 
     flat_col = owner_col * CAP + rank_col
     flat_wide = jnp.concatenate([flat_col] * (slots // 128), axis=1)
@@ -227,35 +251,66 @@
     earlier = jnp.where(same & (iota(same.shape, 0) < iota(same.shape, 1)), 1.0, 0.0)
     rank_row = jnp.sum(earlier, axis=0, keepdims=True).astype(jnp.int32)
     flat_row = owner_row * CAP + rank_row
-    scatter_hot = jnp.where(flat_row == iota((slots, rank_size), 0), 1.0, 0.0).astype(BF16)
-    pick = jnp.where(owner_col == iota((rank_size, 128), 1), 1.0, 0.0).astype(BF16)
-    lanes = iota((rank_size, 128), 1)
-    mine = lax.rem(lanes, 24) // 3 == rank_col
+    scatter_hot[...] = jnp.where(flat_row == iota((slots, rank_size), 0), 1.0, 0.0).astype(BF16)
+
+    for copy in nb_copies:
+        copy.wait_recv()
+    omega_t[...] = jnp.transpose(omega_ref[...])
+
+    @pl.when(me > 0)
+    def _():
+        side = nbc[0]
+        near([side[k : k + 1, :] for k in range(3)], nbw[0], False)
 
     @pl.when(me < nodes - 1)
     def _():
         side = nbc[1]
         near([side[k : k + 1, :] for k in range(3)], nbw[1], False)
 
-    await_bytes(cin, nodes - 1, recv_sem.at[2])
-    found = dot(pick, cin[...].reshape(nodes, 128).astype(BF16))
-    skel_cols = [
-        jnp.sum(jnp.where(mine & (lanes // 24 == k), found, 0.0), axis=1, keepdims=True) for k in range(3)
-    ]
-    skel_tile = kernel_tile(skel_cols, own_rows)
-    transposed = dot(skel_tile, omega_ref[...]).astype(BF16)
-    pout[...] = dot(scatter_hot, transposed).reshape(nodes, CAP, samp).astype(BF16)
-    exchange(pout, pin, 4)
+    def send_rows():
+        await_bytes(asked, nodes - 1, recv_sem.at[1])
+        spread = jnp.broadcast_to(asked[...], (nodes, CAP, 128))
+        spread = jnp.where(iota(spread.shape, 2) == iota(spread.shape, 1), spread, 0.0)
+        flat = jnp.sum(spread.reshape(slots, 128), axis=1, keepdims=True)
+        hot[...] = jnp.where(flat == (iota((slots, leaf), 1) + 1).astype(F32), 1.0, 0.0).astype(BF16)
+        rout[...] = dot(hot[...], omega_ref[...]).reshape(nodes, CAP, samp).astype(BF16)
+        exchange(rout, rin, 3)
+
+    def send_products():
+        await_bytes(zin, planes - 1, recv_sem.at[6])
+        points = jnp.concatenate([zin[i] for i in range(planes)], axis=1)
+        points = jnp.concatenate([points, jnp.zeros((5, slots), F32)], axis=0)
+        parts = jnp.concatenate(split3(points) + (jnp.zeros((8, slots), F32),), axis=0).astype(BF16)
+        picked = dot(parts, scatter_hot[...])
+        skel = picked[0:8] + picked[8:16] + picked[16:24]
+        skel_rows = [skel[k : k + 1, :] for k in range(3)]
+        for m in range(leaf // 128):
+            part = pl.ds(m * 128, 128)
+            columns = [jnp.concatenate([own_wide[k, part, :]] * (rank_size // 128), axis=1) for k in range(3)]
+            tile[part, :] = kernel_tile(columns, skel_rows)
+        transposed = dot(omega_t[...], tile[...]).astype(BF16)
+        pout[...] = dot_nt(scatter_hot[...], transposed).reshape(nodes, CAP, samp).astype(BF16)
+        exchange(pout, pin, 4)
+
+    if ROWS_FIRST:
+        send_rows()
+        send_products()
+    else:
+        send_products()
+        send_rows()
     spots[...] = jnp.transpose(hot[...])
 
     await_bytes(rin, nodes - 1, recv_sem.at[3])
     got = rin[...].astype(F32).reshape(slots, samp).astype(BF16)
     skel_samples = dot(gather_hot, got).astype(BF16)
-    row_ref[...] = (acc[...] + dot_tn(skel_tile, skel_samples)).astype(BF16)
+    row_ref[...] = (acc[...] + dot(tile[...], skel_samples)).astype(BF16)
 
     await_bytes(lists, reps - 1, send_sem.at[0])
-    for which, ref in ((1, reqs), (2, cout), (3, rout), (4, pout)):
+    await_bytes(line, LINE - 1, send_sem.at[5])
+    for which, ref in ((1, reqs), (3, rout), (4, pout)):
         await_bytes(ref, nodes - 1, send_sem.at[which])
+    for which, ref in ((2, zreq), (6, zout)):
+        await_bytes(ref, planes - 1, send_sem.at[which])
     for copy in nb_copies:
         copy.wait_send()
     await_bytes(pin, nodes - 1, recv_sem.at[4])
@@ -300,27 +355,35 @@
                 pltpu.VMEM((reps, 1, share), jnp.int32),
                 pltpu.VMEM((nodes, 1, 128), F32),
                 pltpu.VMEM((nodes, 1, 128), F32),
-                pltpu.VMEM((nodes, 1, 128), F32),
-                pltpu.VMEM((nodes, 1, 128), F32),
+                pltpu.VMEM((nodes // LINE, 1, 128), F32),
+                pltpu.VMEM((nodes // LINE, 1, 128), F32),
+                pltpu.VMEM((nodes // LINE, 3, 128), F32),
+                pltpu.VMEM((nodes // LINE, 3, 128), F32),
+                pltpu.VMEM((LINE, 3, leaf), F32),
                 pltpu.VMEM((nodes, CAP, samp), BF16),
                 pltpu.VMEM((nodes, CAP, samp), BF16),
                 pltpu.VMEM((nodes, CAP, samp), BF16),
                 pltpu.VMEM((2, 3, leaf), F32),
                 pltpu.VMEM((2, leaf, samp), BF16),
                 pltpu.VMEM((leaf, 128), F32),
+                pltpu.VMEM((3, leaf, 128), F32),
+                pltpu.VMEM((samp, leaf), BF16),
+                pltpu.VMEM((9 * LINE, leaf), BF16),
                 pltpu.VMEM((leaf, samp), F32),
                 pltpu.VMEM((nodes * CAP, leaf), BF16),
+                pltpu.VMEM((nodes * CAP, share * reps), BF16),
+                pltpu.VMEM((leaf, share * reps), BF16),
                 pltpu.SemaphoreType.DMA((3,)),
                 pltpu.SemaphoreType.REGULAR,
-                pltpu.SemaphoreType.DMA((5,)),
-                pltpu.SemaphoreType.DMA((5,)),
+                pltpu.SemaphoreType.DMA((7,)),
+                pltpu.SemaphoreType.DMA((7,)),
                 pltpu.SemaphoreType.DMA((2, 2)),
                 pltpu.SemaphoreType.DMA((2, 2)),
             ],
             compiler_params=pltpu.CompilerParams(
                 collective_id=0, has_side_effects=True, vmem_limit_bytes=VMEM_LIMIT
             ),
-        )(coords, omega, skeleton)
+        )(*(pltpu.with_memory_space_constraint(a, pltpu.HBM) for a in (coords, omega, skeleton)))
         return pl.pallas_call(
             finish_kernel,
             out_shape=(

time: 49.9 us -> 44.6 us (0.89)
  Pallas kernels: 46.8 us -> 43.9 us
  local copies, waits for them, and re-layouts: 2.25 us -> 0 us
    pallas_call x1, Pallas kernels: 45.6 us -> 42.7 us  [on_device(): pl.pallas_call(functools.partial(level_kernel, nodes, reps), out_shape=(j...]
    unnamed x6 -> x0, local copies, waits for them, and re-layouts: 2.25 us -> none
where the time goes in v3:
time: 44.6 us; the launch traced here: 44.5 us
  Pallas kernels  43.9 us (98%)
  between operations  0.64 us (1%)
    pallas_call x1, Pallas kernels, on_device(): pl.pallas_call(functools.partial(level_kernel, nodes, reps), out_shape=(j...  42.7 us
    pallas_call x1, Pallas kernels, on_device(): pl.pallas_call(finish_kernel, out_shape=(jax.ShapeDtypeStruct((leaf, samp...  1.14 us

profile of v3, /device:TPU:1, one launch (start us, length us, event | category | flops | bytes accessed | tf_op | source)
XLA Modules:
  0.0 44.5 jit_solution(15644993038130760272)
XLA Ops:
  0.6 42.7 %shard_map.50 = (bf16[512,128]{1,0:T(8,128)(2,1)S(1)}, bf16[128,8,128]{2,1,0:T(8,128)(2,1)S(1)}, bf16[512,1024]{1,0:T(8,128)(2,1)S(1)}) custom-call(f32[3,512]{1,0:T(4,128)} %coords_hbm.1, bf16[512,128]{1,0:T(8,128)(2,1)} %omega_hbm.1, s32[1,64]{1,0:T(1,128)} %skel_hbm.1), custom_call_target="tpu_custom_call" | custom-call | tf_op jit(solution)/shard_map/pallas_call | solution.py:342
  43.4 1.1 %shard_map.51 = (bf16[512,128]{1,0:T(8,128)(2,1)}, f32[512,128]{1,0:T(8,128)}) custom-call(bf16[512,128]{1,0:T(8,128)(2,1)S(1)} %get-tuple-element.5.row_ref, bf16[128,8,128]{2,1,0:T(8,128)(2,1)S(1)} %get-tuple-element.6.pin, bf16[512,1024]{1,0:T(8,128)(2,1)S(1)} %get-tuple-element.7.spots), custom_call_target="tpu_custom_call" | custom-call | tf_op jit(solution)/shard_map/pallas_call | solution.py:387

commit v4 on v3

--- a/solution.py
+++ b/solution.py
@@ -14,7 +14,9 @@
 LINE = 16
 Y_ORDER = (8, 7, 9, 6, 10, 5, 11, 4, 12, 3, 13, 2, 14, 1, 15)
 Z_ORDER = (4, 3, 5, 2, 6, 1, 7)
-ROWS_FIRST = True
+FAR = (4, 3, -3, 2, -2, 1, -1, 0)
+REQUEST_ORDER = (0, 1, -1, 2, -2, 3, -3, 4)
+ROW_ORDER = (0, 1, -1, 2, -2, 3, -3, 4)
 VMEM_LIMIT = 24 << 20
 F32 = jnp.float32
 BF16 = jnp.bfloat16
@@ -73,7 +75,7 @@
     nodes, reps, coords_hbm, omega_hbm, skel_hbm, row_ref, pin, spots,
     coords_ref, omega_ref, skel_ref, lists, reqs, asked, zreq, zasked, zout, zin, line, rout, rin, pout,
     nbc, nbw, own_t, own_wide, omega_t, table, acc, hot, scatter_hot, tile,
-    load_sem, plane_sem, send_sem, recv_sem, nb_send, nb_recv,
+    gather_hot, load_sem, plane_sem, send_sem, recv_sem, asked_sem, nb_send, nb_recv,
 ):
     me, rep = lax.axis_index("node"), lax.axis_index("rep")
     leaf = coords_ref.shape[1]
@@ -94,24 +96,23 @@
 
     barrier = pltpu.get_barrier_semaphore()
 
-    @pl.loop(1, reps)
-    def _(d):
-        pl.semaphore_signal(barrier, inc=1, device_id=(me, lax.rem(rep + d, reps)), device_id_type=MESH)
-
-    @pl.loop(1, LINE)
-    def _(d):
-        pl.semaphore_signal(barrier, inc=1, device_id=(y_peer(d), rep), device_id_type=MESH)
-
-    @pl.loop(1, planes)
-    def _(d):
-        pl.semaphore_signal(barrier, inc=1, device_id=(z_peer(d) * LINE + spot, rep), device_id_type=MESH)
-
     loads = [
         pltpu.make_async_copy(src, dst, load_sem.at[k])
         for k, (src, dst) in enumerate(((skel_hbm, skel_ref), (coords_hbm, coords_ref), (omega_hbm, omega_ref)))
     ]
     for load in loads:
         load.start()
+
+    def hello(node, column):
+        pl.semaphore_signal(barrier, inc=1, device_id=(node, column), device_id_type=MESH)
+
+    for d in Z_ORDER:
+        hello(z_peer(d) * LINE + spot, rep)
+    for d in Y_ORDER:
+        hello(y_peer(d), rep)
+    for d in range(1, reps):
+        hello(me, lax.rem(rep + d, reps))
+
     loads[0].wait()
     loads[1].wait()
     pl.semaphore_wait(barrier, reps - 1 + LINE - 1 + planes - 1)
@@ -121,15 +122,13 @@
             src_ref=skel_ref, dst_ref=lists.at[rep], send_sem=send_sem.at[0], recv_sem=recv_sem.at[0],
             device_id=(me, lax.rem(rep + d, reps)), device_id_type=MESH,
         ).start()
+    for d in Z_ORDER:
+        pl.semaphore_signal(plane_sem, inc=1, device_id=(z_peer(d) * LINE + spot, rep), device_id_type=MESH)
     for d in Y_ORDER:
         pltpu.make_async_remote_copy(
             src_ref=coords_ref, dst_ref=line.at[spot], send_sem=send_sem.at[5], recv_sem=recv_sem.at[5],
             device_id=(y_peer(d), rep), device_id_type=MESH,
         ).start()
-
-    @pl.loop(1, planes)
-    def _(d):
-        pl.semaphore_signal(plane_sem, inc=1, device_id=(z_peer(d) * LINE + spot, rep), device_id_type=MESH)
 
     loads[2].wait()
     lists[rep] = skel_ref[...]
@@ -167,18 +166,21 @@
         view = ref.at[pl.ds(0, count)]
         pltpu.make_async_copy(view, view, sem).wait()
 
+    def send_to(src, dst, target, out_sem, in_sem):
+        pltpu.make_async_remote_copy(
+            src_ref=src.at[target], dst_ref=dst.at[me], send_sem=out_sem, recv_sem=in_sem,
+            device_id=(target, rep), device_id_type=MESH,
+        ).start()
+
+    def send_pair(src, dst, chip, out_sem, in_sem, own_chip):
+        if not own_chip:
+            send_to(src, dst, chip + core, out_sem, in_sem)
+        send_to(src, dst, chip + 1 - core, out_sem, in_sem)
+
     def exchange(src, dst, which):
-        def send(target):
-            pltpu.make_async_remote_copy(
-                src_ref=src.at[target], dst_ref=dst.at[me], send_sem=send_sem.at[which], recv_sem=recv_sem.at[which],
-                device_id=(target, rep), device_id_type=MESH,
-            ).start()
-
-        for dy, dz in offsets:
-            base = lax.rem(z + (dz + 8), 8) * LINE + lax.rem(y + (dy + 8), 8) * 2
-            send(base + core)
-            send(base + 1 - core)
-        send(z * LINE + y * 2 + 1 - core)
+        for dy, dz in offsets + [(0, 0)]:
+            chip = lax.rem(z + (dz + 8), 8) * LINE + lax.rem(y + (dy + 8), 8) * 2
+            send_pair(src, dst, chip, send_sem.at[which], recv_sem.at[which], dy == 0 and dz == 0)
 
     def z_exchange(src, dst, which):
         for d in Z_ORDER:
@@ -217,7 +219,11 @@
     owner_hot = jnp.where(owner_row == iota((nodes, rank_size), 0), 1.0, 0.0).astype(BF16)
     reqs[...] = requests(rank_col, owner_hot).reshape(nodes, 1, 128)
     pl.semaphore_wait(plane_sem, planes - 1)
-    exchange(reqs, asked, 1)
+    for dz in REQUEST_ORDER:
+        base = z_peer(planes + dz) * LINE
+        for dy in FAR:
+            chip = base + lax.rem(y + (dy + 8), 8) * 2
+            send_pair(reqs, asked, chip, send_sem.at[1], asked_sem.at[z], dy == 0 and dz == 0)
     for copy in nb_copies:
         copy.start()
 
@@ -225,6 +231,16 @@
     for k in range(3):
         for part, values in enumerate(split3(jnp.concatenate([line[n, k : k + 1, :] for n in range(LINE)], axis=0))):
             table[pl.ds((3 * k + part) * LINE, LINE), :] = values.astype(BF16)
+
+    flat_col = owner_col * CAP + rank_col
+    flat_wide = jnp.concatenate([flat_col] * (slots // 128), axis=1)
+    gather_hot[...] = jnp.where(flat_wide == iota((rank_size, slots), 1), 1.0, 0.0).astype(BF16)
+    earlier = jnp.where(same & (iota(same.shape, 0) < iota(same.shape, 1)), 1.0, 0.0)
+    rank_row = jnp.sum(earlier, axis=0, keepdims=True).astype(jnp.int32)
+    flat_row = owner_row * CAP + rank_row
+    scatter_hot[...] = jnp.where(flat_row == iota((slots, rank_size), 0), 1.0, 0.0).astype(BF16)
+
+    omega_t[...] = jnp.transpose(omega_ref[...])
 
     await_bytes(zasked, planes - 1, recv_sem.at[2])
     width = 256
@@ -245,36 +261,21 @@
     z_exchange(zout, zin, 6)
     zin[z] = zout[z]
 
-    flat_col = owner_col * CAP + rank_col
-    flat_wide = jnp.concatenate([flat_col] * (slots // 128), axis=1)
-    gather_hot = jnp.where(flat_wide == iota((rank_size, slots), 1), 1.0, 0.0).astype(BF16)
-    earlier = jnp.where(same & (iota(same.shape, 0) < iota(same.shape, 1)), 1.0, 0.0)
-    rank_row = jnp.sum(earlier, axis=0, keepdims=True).astype(jnp.int32)
-    flat_row = owner_row * CAP + rank_row
-    scatter_hot[...] = jnp.where(flat_row == iota((slots, rank_size), 0), 1.0, 0.0).astype(BF16)
-
-    for copy in nb_copies:
-        copy.wait_recv()
-    omega_t[...] = jnp.transpose(omega_ref[...])
-
-    @pl.when(me > 0)
-    def _():
-        side = nbc[0]
-        near([side[k : k + 1, :] for k in range(3)], nbw[0], False)
-
-    @pl.when(me < nodes - 1)
-    def _():
-        side = nbc[1]
-        near([side[k : k + 1, :] for k in range(3)], nbw[1], False)
-
-    def send_rows():
-        await_bytes(asked, nodes - 1, recv_sem.at[1])
-        spread = jnp.broadcast_to(asked[...], (nodes, CAP, 128))
+    point = (iota((LINE * CAP, leaf), 1) + 1).astype(F32)
+    for dz in ROW_ORDER:
+        zs = z_peer(planes + dz)
+        nodes_of = pl.ds(pl.multiple_of(zs * LINE, LINE), LINE)
+        slots_of = pl.ds(pl.multiple_of(zs * LINE * CAP, LINE * CAP), LINE * CAP)
+        await_bytes(asked, LINE if dz else LINE - 1, asked_sem.at[zs])
+        spread = jnp.broadcast_to(asked[nodes_of], (LINE, CAP, 128))
         spread = jnp.where(iota(spread.shape, 2) == iota(spread.shape, 1), spread, 0.0)
-        flat = jnp.sum(spread.reshape(slots, 128), axis=1, keepdims=True)
-        hot[...] = jnp.where(flat == (iota((slots, leaf), 1) + 1).astype(F32), 1.0, 0.0).astype(BF16)
-        rout[...] = dot(hot[...], omega_ref[...]).reshape(nodes, CAP, samp).astype(BF16)
-        exchange(rout, rin, 3)
+        flat = jnp.sum(spread.reshape(LINE * CAP, 128), axis=1, keepdims=True)
+        point_hot = jnp.where(flat == point, 1.0, 0.0).astype(BF16)
+        hot[slots_of, :] = point_hot
+        rout[nodes_of] = dot(point_hot, omega_ref[...]).reshape(LINE, CAP, samp).astype(BF16)
+        for dy in FAR:
+            chip = zs * LINE + lax.rem(y + (dy + 8), 8) * 2
+            send_pair(rout, rin, chip, send_sem.at[3], recv_sem.at[3], dy == 0 and dz == 0)
 
     def send_products():
         await_bytes(zin, planes - 1, recv_sem.at[6])
@@ -292,17 +293,26 @@
         pout[...] = dot_nt(scatter_hot[...], transposed).reshape(nodes, CAP, samp).astype(BF16)
         exchange(pout, pin, 4)
 
-    if ROWS_FIRST:
-        send_rows()
-        send_products()
-    else:
-        send_products()
-        send_rows()
+    send_products()
+
+    for copy in nb_copies:
+        copy.wait_recv()
+
+    @pl.when(me > 0)
+    def _():
+        side = nbc[0]
+        near([side[k : k + 1, :] for k in range(3)], nbw[0], False)
+
+    @pl.when(me < nodes - 1)
+    def _():
+        side = nbc[1]
+        near([side[k : k + 1, :] for k in range(3)], nbw[1], False)
+
     spots[...] = jnp.transpose(hot[...])
 
     await_bytes(rin, nodes - 1, recv_sem.at[3])
     got = rin[...].astype(F32).reshape(slots, samp).astype(BF16)
-    skel_samples = dot(gather_hot, got).astype(BF16)
+    skel_samples = dot(gather_hot[...], got).astype(BF16)
     row_ref[...] = (acc[...] + dot(tile[...], skel_samples)).astype(BF16)
 
     await_bytes(lists, reps - 1, send_sem.at[0])
@@ -373,10 +383,12 @@
                 pltpu.VMEM((nodes * CAP, leaf), BF16),
                 pltpu.VMEM((nodes * CAP, share * reps), BF16),
                 pltpu.VMEM((leaf, share * reps), BF16),
+                pltpu.VMEM((share * reps, nodes * CAP), BF16),
                 pltpu.SemaphoreType.DMA((3,)),
                 pltpu.SemaphoreType.REGULAR,
                 pltpu.SemaphoreType.DMA((7,)),
                 pltpu.SemaphoreType.DMA((7,)),
+                pltpu.SemaphoreType.DMA((nodes // LINE,)),
                 pltpu.SemaphoreType.DMA((2, 2)),
                 pltpu.SemaphoreType.DMA((2, 2)),
             ],

time: 44.6 us -> 42.9 us (0.962)
  Pallas kernels: 43.9 us -> 42.1 us
    pallas_call x1, Pallas kernels: 42.7 us -> 41 us  [on_device(): pl.pallas_call(functools.partial(level_kernel, nodes, reps), out_shape=(j...]
where the time goes in v4:
time: 42.9 us; the launch traced here: 42.8 us
  Pallas kernels  42.1 us (98%)
  between operations  0.64 us (1%)
    pallas_call x1, Pallas kernels, on_device(): pl.pallas_call(functools.partial(level_kernel, nodes, reps), out_shape=(j...  41 us
    pallas_call x1, Pallas kernels, on_device(): pl.pallas_call(finish_kernel, out_shape=(jax.ShapeDtypeStruct((leaf, samp...  1.14 us

profile of v4, /device:TPU:1, one launch (start us, length us, event | category | flops | bytes accessed | tf_op | source)
XLA Modules:
  0.0 42.8 jit_solution(37514261190805209)
XLA Ops:
  0.6 41.0 %shard_map.50 = (bf16[512,128]{1,0:T(8,128)(2,1)S(1)}, bf16[128,8,128]{2,1,0:T(8,128)(2,1)S(1)}, bf16[512,1024]{1,0:T(8,128)(2,1)S(1)}) custom-call(f32[3,512]{1,0:T(4,128)} %coords_hbm.1, bf16[512,128]{1,0:T(8,128)(2,1)} %omega_hbm.1, s32[1,64]{1,0:T(1,128)} %skel_hbm.1), custom_call_target="tpu_custom_call" | custom-call | tf_op jit(solution)/shard_map/pallas_call | solution.py:352
  41.6 1.1 %shard_map.51 = (bf16[512,128]{1,0:T(8,128)(2,1)}, f32[512,128]{1,0:T(8,128)}) custom-call(bf16[512,128]{1,0:T(8,128)(2,1)S(1)} %get-tuple-element.5.row_ref, bf16[128,8,128]{2,1,0:T(8,128)(2,1)S(1)} %get-tuple-element.6.pin, bf16[512,1024]{1,0:T(8,128)(2,1)S(1)} %get-tuple-element.7.spots), custom_call_target="tpu_custom_call" | custom-call | tf_op jit(solution)/shard_map/pallas_call | solution.py:399

commit v5 on v4

--- a/solution.py
+++ b/solution.py
@@ -68,7 +68,8 @@
             if group:
                 groups.append(group)
     groups.sort(key=lambda g: -(abs(g[0][0]) + abs(g[0][1])))
-    return [pair for group in groups for pair in group]
+    flat = [pair for group in groups for pair in group]
+    return sorted(flat, key=lambda p: -(2 * abs(p[0]) + abs(p[1])))
 
 
 def level_kernel(
@@ -112,10 +113,12 @@
         hello(y_peer(d), rep)
     for d in range(1, reps):
         hello(me, lax.rem(rep + d, reps))
+    for d in (1, nodes - 1):
+        hello(lax.rem(me + d, nodes), rep)
 
     loads[0].wait()
     loads[1].wait()
-    pl.semaphore_wait(barrier, reps - 1 + LINE - 1 + planes - 1)
+    pl.semaphore_wait(barrier, reps - 1 + LINE - 1 + planes - 1 + 2)
 
     for d in range(1, reps):
         pltpu.make_async_remote_copy(
@@ -130,7 +133,19 @@
             device_id=(y_peer(d), rep), device_id_type=MESH,
         ).start()
 
+    nb_copies = []
+    for side, step in ((0, 1), (1, nodes - 1)):
+        for j, (src, dst) in enumerate(((coords_ref, nbc), (omega_ref, nbw))):
+            nb_copies.append(
+                pltpu.make_async_remote_copy(
+                    src_ref=src, dst_ref=dst.at[side], send_sem=nb_send.at[side, j], recv_sem=nb_recv.at[side, j],
+                    device_id=(lax.rem(me + step, nodes), rep), device_id_type=MESH,
+                )
+            )
     loads[2].wait()
+    for copy in nb_copies:
+        copy.start()
+
     lists[rep] = skel_ref[...]
     line[spot] = coords_ref[...]
     asked[me] = jnp.zeros((1, 128), F32)
@@ -151,16 +166,6 @@
             acc[part, :] = term if first else acc[part, :] + term
 
     near(own_rows, omega_ref[...], True)
-
-    nb_copies = []
-    for side, step in ((0, 1), (1, nodes - 1)):
-        for j, (src, dst) in enumerate(((coords_ref, nbc), (omega_ref, nbw))):
-            nb_copies.append(
-                pltpu.make_async_remote_copy(
-                    src_ref=src, dst_ref=dst.at[side], send_sem=nb_send.at[side, j], recv_sem=nb_recv.at[side, j],
-                    device_id=(lax.rem(me + step, nodes), rep), device_id_type=MESH,
-                )
-            )
 
     def await_bytes(ref, count, sem):
         view = ref.at[pl.ds(0, count)]
@@ -224,8 +229,6 @@
         for dy in FAR:
             chip = base + lax.rem(y + (dy + 8), 8) * 2
             send_pair(reqs, asked, chip, send_sem.at[1], asked_sem.at[z], dy == 0 and dz == 0)
-    for copy in nb_copies:
-        copy.start()
 
     await_bytes(line, LINE - 1, recv_sem.at[5])
     for k in range(3):

time: 42.9 us -> 42.7 us (level)
  no operation moved by 1% of the time
where the time goes in v5:
time: 42.7 us; the launch traced here: 42.6 us
  Pallas kernels  41.9 us (98%)
  between operations  0.64 us (1%)
    pallas_call x1, Pallas kernels, on_device(): pl.pallas_call(functools.partial(level_kernel, nodes, reps), out_shape=(j...  40.8 us
    pallas_call x1, Pallas kernels, on_device(): pl.pallas_call(finish_kernel, out_shape=(jax.ShapeDtypeStruct((leaf, samp...  1.14 us

profile of v5, /device:TPU:1, one launch (start us, length us, event | category | flops | bytes accessed | tf_op | source)
XLA Modules:
  0.0 42.6 jit_solution(7063679738641646338)
XLA Ops:
  0.6 40.8 %shard_map.50 = (bf16[512,128]{1,0:T(8,128)(2,1)S(1)}, bf16[128,8,128]{2,1,0:T(8,128)(2,1)S(1)}, bf16[512,1024]{1,0:T(8,128)(2,1)S(1)}) custom-call(f32[3,512]{1,0:T(4,128)} %coords_hbm.1, bf16[512,128]{1,0:T(8,128)(2,1)} %omega_hbm.1, s32[1,64]{1,0:T(1,128)} %skel_hbm.1), custom_call_target="tpu_custom_call" | custom-call | tf_op jit(solution)/shard_map/pallas_call | solution.py:355
  41.4 1.1 %shard_map.51 = (bf16[512,128]{1,0:T(8,128)(2,1)}, f32[512,128]{1,0:T(8,128)}) custom-call(bf16[512,128]{1,0:T(8,128)(2,1)S(1)} %get-tuple-element.5.row_ref, bf16[128,8,128]{2,1,0:T(8,128)(2,1)S(1)} %get-tuple-element.6.pin, bf16[512,1024]{1,0:T(8,128)(2,1)S(1)} %get-tuple-element.7.spots), custom_call_target="tpu_custom_call" | custom-call | tf_op jit(solution)/shard_map/pallas_call | solution.py:402

commit v6 on v5

--- a/solution.py
+++ b/solution.py
@@ -280,6 +280,14 @@
             chip = zs * LINE + lax.rem(y + (dy + 8), 8) * 2
             send_pair(rout, rin, chip, send_sem.at[3], recv_sem.at[3], dy == 0 and dz == 0)
 
+    for copy in nb_copies:
+        copy.wait_recv()
+
+    @pl.when(me > 0)
+    def _():
+        side = nbc[0]
+        near([side[k : k + 1, :] for k in range(3)], nbw[0], False)
+
     def send_products():
         await_bytes(zin, planes - 1, recv_sem.at[6])
         points = jnp.concatenate([zin[i] for i in range(planes)], axis=1)
@@ -297,14 +305,6 @@
         exchange(pout, pin, 4)
 
     send_products()
-
-    for copy in nb_copies:
-        copy.wait_recv()
-
-    @pl.when(me > 0)
-    def _():
-        side = nbc[0]
-        near([side[k : k + 1, :] for k in range(3)], nbw[0], False)
 
     @pl.when(me < nodes - 1)
     def _():

time: 42.7 us -> 42.6 us (level)
  no operation moved by 1% of the time
where the time goes in v6:
time: 42.6 us; the launch traced here: 42.5 us
  Pallas kernels  41.9 us (98%)
  between operations  0.64 us (2%)
    pallas_call x1, Pallas kernels, on_device(): pl.pallas_call(functools.partial(level_kernel, nodes, reps), out_shape=(j...  40.7 us
    pallas_call x1, Pallas kernels, on_device(): pl.pallas_call(finish_kernel, out_shape=(jax.ShapeDtypeStruct((leaf, samp...  1.14 us

profile of v6, /device:TPU:1, one launch (start us, length us, event | category | flops | bytes accessed | tf_op | source)
XLA Modules:
  0.0 42.5 jit_solution(13419497142323768576)
XLA Ops:
  0.6 40.7 %shard_map.50 = (bf16[512,128]{1,0:T(8,128)(2,1)S(1)}, bf16[128,8,128]{2,1,0:T(8,128)(2,1)S(1)}, bf16[512,1024]{1,0:T(8,128)(2,1)S(1)}) custom-call(f32[3,512]{1,0:T(4,128)} %coords_hbm.1, bf16[512,128]{1,0:T(8,128)(2,1)} %omega_hbm.1, s32[1,64]{1,0:T(1,128)} %skel_hbm.1), custom_call_target="tpu_custom_call" | custom-call | tf_op jit(solution)/shard_map/pallas_call | solution.py:355
  41.4 1.1 %shard_map.51 = (bf16[512,128]{1,0:T(8,128)(2,1)}, f32[512,128]{1,0:T(8,128)}) custom-call(bf16[512,128]{1,0:T(8,128)(2,1)S(1)} %get-tuple-element.5.row_ref, bf16[128,8,128]{2,1,0:T(8,128)(2,1)S(1)} %get-tuple-element.6.pin, bf16[512,1024]{1,0:T(8,128)(2,1)S(1)} %get-tuple-element.7.spots), custom_call_target="tpu_custom_call" | custom-call | tf_op jit(solution)/shard_map/pallas_call | solution.py:402
